TPU v7x, 32 devices: a whole 2x2x4 slice. The times are simulated.
32 devices in a mesh: ga: 2 (over x), ta: 4 (over y, core), gy: 4 (over z).
Axes of the slice: x: 2, y: 2, z: 4, core: 2. Of those that a mesh axis runs over, the one named last changes fastest.
Arguments:
- clip: bfloat16 [32, 16, 64, 512], P(('ga', 'ta'), 'gy'), parts along dimension 0, may hold values from -6 to 6
- w_space: bfloat16 [3, 3, 512, 512], replicated, may hold values from -0.09375 to 0.09375
- w_time: bfloat16 [3, 512, 512], replicated, may hold values from -0.15625 to 0.15625
- w_qkv: bfloat16 [512, 1536], replicated, may hold values from -0.61871843 to 0.61871843
- w_out: bfloat16 [512, 512], replicated, may hold values from -0.25 to 0.25
- norm_gain: float32 [512], replicated, may hold values from 0.1 to 1.9
Outputs:
- block_out: bfloat16 [32, 16, 64, 512], P(('ga', 'ta'), 'gy'), parts along dimension 0
There are 2 independent parts, one for each index of `ga`. A program takes and returns all parts, laid end to end along the dimension named above; an argument that names none is the same for every part. Nothing has to cross between parts.
All inputs are finite; a program needn't handle non-finite values.
Results may differ from a plain program's by a relative error of at most 0.0085.
Values may be sent and summed in bfloat16 or wider, within the bound.
No kernel may reach another device: no remote copies, remote signals or barrier semaphores. Data moves between devices by JAX's collectives and lax.ppermute only.
A program may use at most 64 MiB of HBM per device.

v0:
```python
import jax
import jax.numpy as jnp
from jax import lax
from jax.sharding import PartitionSpec as P

HEADS = 8


def padded_2(block, sides, width):
    for axis, dim in sides:
        count = lax.axis_size(axis)
        forward = [(i, i + 1) for i in range(count - 1)]
        backward = [(target, source) for source, target in forward]
        low = lax.ppermute(
            lax.slice_in_dim(block, block.shape[dim] - width, None, axis=dim), axis, forward
        )
        high = lax.ppermute(lax.slice_in_dim(block, 0, width, axis=dim), axis, backward)
        block = jnp.concatenate([low, block, high], axis=dim)
    return block


def from_behind(array, axis, by):
    devices = lax.axis_size(axis)
    pairs = [(i, i + by) for i in range(devices) if 0 <= i + by < devices]
    return lax.ppermute(array, axis, pairs)


def conv_space(padded, w_space, height, width):
    channels = padded.shape[-1]
    total = jnp.zeros(padded.shape[:1] + (height, width, channels), jnp.float32)
    for row_off in range(3):
        for col_off in range(3):
            window = padded[:, row_off : row_off + height, col_off : col_off + width, :]
            product = jnp.dot(
                window.reshape(-1, channels),
                w_space[row_off, col_off],
                preferred_element_type=jnp.float32,
            )
            total = total + product.reshape(total.shape)
    return total


def temporal_mix(clip, hidden, earlier, w_time, norm_gain):
    channels = clip.shape[-1]
    frames = hidden.shape[0]
    joined = jnp.concatenate([earlier, hidden], axis=0)
    total = jnp.zeros(hidden.shape, jnp.float32)
    for tap_index in range(3):
        window = joined[2 - tap_index : 2 - tap_index + frames]
        product = jnp.dot(
            window.reshape(-1, channels), w_time[tap_index], preferred_element_type=jnp.float32
        )
        total = total + product.reshape(hidden.shape)
    mixed = (clip.astype(jnp.float32) + total).astype(jnp.bfloat16)
    wide = mixed.astype(jnp.float32)
    scale = lax.rsqrt(jnp.mean(wide * wide, axis=-1, keepdims=True) + 1e-06)
    normed = (wide * scale * norm_gain).astype(jnp.bfloat16)
    return (mixed, normed)


def project(normed, w_qkv):
    channels = normed.shape[-1]
    flattened = jnp.dot(
        normed.reshape(-1, channels), w_qkv, preferred_element_type=jnp.float32
    ).astype(jnp.bfloat16)
    joined = flattened.reshape(normed.shape[:-1] + (3 * channels,))
    return (
        joined[..., :channels],
        joined[..., channels : 2 * channels],
        joined[..., 2 * channels :],
    )


def attend(queries, keyset, valueset, heads):
    frames, rows, cols, channels = queries.shape
    head_dim = channels // heads
    shape = (frames, rows, cols, heads, head_dim)
    scores = jnp.einsum(
        "frwhd,grwhd->rwhfg",
        queries.reshape(shape),
        keyset.reshape(shape),
        preferred_element_type=jnp.float32,
    )
    scores = scores * (1.0 / head_dim**0.5)
    peak = jnp.max(scores, axis=-1, keepdims=True)
    expo = jnp.exp(scores - peak)
    probs = (expo / jnp.sum(expo, axis=-1, keepdims=True)).astype(jnp.bfloat16)
    output = jnp.einsum(
        "rwhfg,grwhd->frwhd", probs, valueset.reshape(shape), preferred_element_type=jnp.float32
    )
    return output.reshape(queries.shape).astype(jnp.bfloat16)


def attend_back(queries, keyset, valueset):
    output = attend(queries, keyset, valueset, HEADS)
    return lax.all_to_all(output, "ta", split_axis=0, concat_axis=2, tiled=True)


def per_device(clip, w_space, w_time, w_qkv, w_out, norm_gain):
    frames, height, width, channels = clip.shape
    rimmed = padded_2(clip, (("gy", 1),), 1)
    padded = jnp.pad(rimmed, ((0, 0), (0, 0), (1, 1), (0, 0)))
    hidden = jax.nn.silu(conv_space(padded, w_space, height, width)).astype(jnp.bfloat16)
    earlier = from_behind(hidden[-2:], "ta", 1)
    mixed, normed = temporal_mix(clip, hidden, earlier, w_time, norm_gain)
    queries, keyset, valueset = project(
        lax.all_to_all(normed, "ta", split_axis=2, concat_axis=0, tiled=True), w_qkv
    )
    attended = attend_back(queries, keyset, valueset)
    projected = jnp.dot(
        attended.reshape(-1, channels), w_out, preferred_element_type=jnp.float32
    ).reshape(clip.shape)
    return (mixed.astype(jnp.float32) + projected).astype(jnp.bfloat16)


def solution(mesh):
    in_specs = (P(("ga", "ta"), "gy", None, None), P(), P(), P(), P(), P())
    out_specs = P(("ga", "ta"), "gy", None, None)
    return jax.shard_map(
        per_device, mesh=mesh, in_specs=in_specs, out_specs=out_specs, check_vma=False
    )
```

profile of v0, /device:TPU:0, one launch (start us, length us, event | category | flops | bytes accessed | tf_op | source)
XLA Modules:
  0.0 112.8 jit_solution(17687621035857392692)
XLA Ops:
  0.0 0.0 copy-start
  0.0 1.2 %fusion.79 = (bf16[4,1,64,512]{3,2,1,0:T(8,128)(2,1)S(1)}, bf16[4,1,64,512]{3,2,1,0:T(8,128)(2,1)S(1)}) fusion(bf16[4,4,64,512]{3,2,1,0:T(8,128)(2,1)} %param.6), kind=kLoop, calls=%fused_computation.87 | loop fusion | bytes 1048576 | tf_op jit(solution)/shard_map/slice | solution.py:15
  1.2 5.0 %collective-permute-start = (bf16[4,1,64,512]{3,2,1,0:T(8,128)(2,1)S(1)}, bf16[4,1,64,512]{3,2,1,0:T(8,128)(2,1)S(1)}, u32[]{:S(2)}, u32[]{:S(2)}) collective-permute-start(bf16[4,1,64,512]{3,2,1,0:T(8,128)(2,1)S(1)} %get-tuple-element.8), channel_id=1, source_target_pairs={{0,1},{1,2},{2,3},{4,5},{5,6},{6,7},{8,9},{9,10},{10,11},{12,13},{... | collective-permute-start | bytes 786440 | tf_op jit(solution)/shard_map/ppermute | solution.py:14
  6.2 0.0 copy-start.2
  6.2 1.4 %collective-permute-start.1 = (bf16[4,1,64,512]{3,2,1,0:T(8,128)(2,1)S(1)}, bf16[4,1,64,512]{3,2,1,0:T(8,128)(2,1)S(1)}, u32[]{:S(2)}, u32[]{:S(2)}) collective-permute-start(bf16[4,1,64,512]{3,2,1,0:T(8,128)(2,1)S(1)} %get-tuple-element.9), channel_id=1, source_target_pairs={{1,0},{2,1},{3,2},{5,4},{6,5},{7,6},{9,8},{10,9},{11,10},{13,12},{... | collective-permute-start | bytes 786440 | tf_op jit(solution)/shard_map/ppermute | solution.py:17
  7.6 0.0 copy-start.4
  7.6 2.2 %fusion.55 = f32[4,4,64,512]{3,2,1,0:T(8,128)S(1)} fusion(bf16[4,4,64,512]{3,2,1,0:T(8,128)(2,1)} %param.6, bf16[3,3,512,512]{3,2,1,0:T(8,128)(2,1)} %param.7), kind=kOutput, calls=%fused_computation.62 | convolution fusion | flops 536870912 | bytes 3670016 | tf_op jit(solution)/shard_map/dot_general | solution.py:34
  9.8 1.9 %collective-permute-done = bf16[4,1,64,512]{3,2,1,0:T(8,128)(2,1)S(1)} collective-permute-done((bf16[4,1,64,512]{3,2,1,0:T(8,128)(2,1)S(1)}, bf16[4,1,64,512]{3,2,1,0:T(8,128)(2,1)S(1)}, u32[]{:S(2)}, u32[]{:S(2)}) %collective-permute-start) | collective-permute-done | bytes 262176 | tf_op jit(solution)/shard_map/ppermute | solution.py:14
  11.7 4.3 %collective-permute-done.1 = bf16[4,1,64,512]{3,2,1,0:T(8,128)(2,1)S(1)} collective-permute-done((bf16[4,1,64,512]{3,2,1,0:T(8,128)(2,1)S(1)}, bf16[4,1,64,512]{3,2,1,0:T(8,128)(2,1)S(1)}, u32[]{:S(2)}, u32[]{:S(2)}) %collective-permute-start.1) | collective-permute-done | bytes 262176 | tf_op jit(solution)/shard_map/ppermute | solution.py:17
  16.0 0.0 copy-done.2
  16.0 0.9 fusion.22
  16.9 0.0 copy-done.4
  16.9 0.7 fusion.35
  17.6 0.7 fusion.37
  18.3 0.7 fusion.39
  19.0 0.7 fusion.41
  19.8 0.7 fusion.43
  20.5 0.7 fusion.23
  21.2 0.7 fusion.27
  21.9 0.0 copy-start.5
  21.9 1.4 %multiply_convert_fusion = bf16[4,4,64,512]{3,2,1,0:T(8,128)(2,1)S(1)} fusion(f32[4,4,64,512]{3,2,1,0:T(8,128)S(1)} %fusion.27, f32[4,4,64,512]{3,2,1,0:T(8,128)S(1)} %fusion.35, f32[4,4,64,512]{3,2,1,0:T(8,128)S(1)} %fusion.37, f32[4,4,64,512]{3,2,1,0:T(8,128)S(1)} %fusion.55, f32[4,4,64,512]{3,2,1,0:T(8,128)S(1)} %fusion.39, ...), kind=kOutput, calls=%fused_computation.25 | convolution fusion | flops 543686656 | bytes 19398656 | tf_op jit(solution)/shard_map/dot_general | solution.py:34
  23.4 1.3 %collective-permute-start.2 = (bf16[2,4,64,512]{3,2,1,0:T(8,128)(2,1)S(1)}, bf16[2,4,64,512]{3,2,1,0:T(8,128)(2,1)S(1)}, u32[]{:S(2)}, u32[]{:S(2)}) collective-permute-start(bf16[2,4,64,512]{3,2,1,0:T(8,128)(2,1)S(1)} %slice.124), channel_id=1, source_target_pairs={{0,4},{4,8},{8,12},{1,5},{5,9},{9,13},{2,6},{6,10},{10,14},{3,7},{... | collective-permute-start | bytes 1572872 | tf_op jit(solution)/shard_map/ppermute | solution.py:25
  24.7 0.0 copy-done.5
  24.7 0.7 fusion.49
  25.4 0.8 collective-permute-done.2
  26.2 0.7 fusion.45
  26.9 0.0 copy-start.6
  26.9 1.0 fusion.5
  27.9 0.0 copy-done.6
  28.0 0.3 fusion.7
  28.3 0.8 copy.22
  29.1 24.7 %all_to_all.30 = bf16[4,4,64,512]{3,1,0,2:T(4,128)(2,1)S(1)} all-to-all(bf16[4,4,64,512]{3,1,0,2:T(4,128)(2,1)S(1)} %copy.22), channel_id=1, replica_groups=mesh['ga'=2,'ta'=4,'gy'=4] {'ta'}, dimensions={2} | all-to-all | bytes 2097152 | tf_op jit(solution)/shard_map/all_to_all | solution.py:107
  53.8 0.6 copy.23
  54.4 0.1 copy.24
  54.4 0.0 copy-done
  54.5 1.8 %convolution_convert_fusion = bf16[1024,1536]{1,0:T(8,128)(2,1)S(1)} fusion(bf16[1024,512]{1,0:T(8,128)(2,1)S(1)} %bitcast.119, bf16[512,1536]{1,0:T(8,128)(2,1)S(1)} %copy-done), kind=kOutput, calls=%fused_computation.5 | convolution fusion | flops 1612185600 | bytes 5767168 | tf_op jit(solution)/shard_map/dot_general | solution.py:63
  56.3 1.7 %fusion.78 = (bf16[16,4,16,512]{3,2,1,0:T(8,128)(2,1)S(1)}, bf16[16,4,16,512]{3,2,1,0:T(8,128)(2,1)}, bf16[16,4,16,512]{3,2,1,0:T(8,128)(2,1)}) fusion(bf16[16,4,16,1536]{3,2,1,0:T(8,128)(2,1)S(1)} %bitcast.117), kind=kLoop, calls=%fused_computation.86 | loop fusion | bytes 6291456 | tf_op jit(solution)/shard_map/slice | solution.py:70
  57.9 2.1 %reshape.84 = bf16[16,4,16,8,64]{4,3,2,1,0:T(8,128)(2,1)} reshape(bf16[16,4,16,512]{3,2,1,0:T(8,128)(2,1)S(1)} %get-tuple-element.5) | data formatting | bytes 2097152 | tf_op jit(solution)/shard_map/reshape | solution.py:89
  60.0 2.8 %reshape.86 = bf16[16,4,16,8,64]{4,3,2,1,0:T(8,128)(2,1)S(1)} reshape(bf16[16,4,16,512]{3,2,1,0:T(8,128)(2,1)} %get-tuple-element.6) | data formatting | bytes 2097152 | tf_op jit(solution)/shard_map/reshape | solution.py:81
  62.8 3.9 %reshape.85 = bf16[16,4,16,8,64]{4,3,2,1,0:T(8,128)(2,1)} reshape(bf16[16,4,16,512]{3,2,1,0:T(8,128)(2,1)} %get-tuple-element.7) | data formatting | bytes 2097152 | tf_op jit(solution)/shard_map/reshape | solution.py:80
  66.7 4.1 %fusion.11 = f32[4,16,8,16,16]{3,4,2,1,0:T(8,128)S(1)} fusion(bf16[16,4,16,8,64]{4,3,2,1,0:T(8,128)(2,1)S(1)} %reshape.86, bf16[16,4,16,8,64]{4,3,2,1,0:T(8,128)(2,1)} %reshape.85), kind=kOutput, calls=%fused_computation.18 | convolution fusion | flops 16777216 | bytes 2621440 | tf_op jit(solution)/shard_map/frwhd,grwhd->rwhfg/dot_general | solution.py:78
  70.8 0.0 copy-start.3
  70.8 17.7 %fusion.80 = (f32[4,16,8,16]{3,2,1,0:T(8,128)S(1)}, f32[4,16,8,16,16]{3,4,2,1,0:T(8,128)S(1)}) fusion(f32[4,16,8,16,16]{3,4,2,1,0:T(8,128)S(1)} %fusion.11), kind=kOutput, calls=%fused_computation.88 | output fusion | flops 524303 | bytes 1081344 | tf_op jit(solution)/shard_map/sub | solution.py:86
  88.6 0.0 copy-done.3
  88.6 1.7 %convert_bitcast_fusion = bf16[16,4,16,8,64]{4,0,3,2,1:T(8,128)(2,1)S(1)} fusion(f32[4,16,8,16,16]{3,4,2,1,0:T(8,128)S(1)} %get-tuple-element.13, f32[4,16,8,16]{3,2,1,0:T(8,128)S(1)} %get-tuple-element.12, bf16[16,4,16,8,64]{4,3,2,1,0:T(8,128)(2,1)S(1)} %copy-done.3), kind=kOutput, calls=%fused_computation.21 | convolution fusion | flops 17563648 | bytes 2654208 | tf_op jit(solution)/shard_map/rwhfg,grwhd->frwhd/dot_general | solution.py:88
  90.3 0.5 copy.29
  90.9 2.0 %convert_element_type.45 = bf16[16,4,16,512]{3,2,1,0:T(8,128)(2,1)} reshape(bf16[16,4,16,8,64]{4,3,2,1,0:T(8,128)(2,1)S(1)} %copy.29) | data formatting | bytes 2097152 | tf_op jit(solution)/shard_map/convert_element_type | solution.py:91
  92.9 0.0 copy-start.7
  92.9 18.0 %all_to_all.31 = bf16[16,4,16,512]{3,2,1,0:T(8,128)(2,1)S(1)} all-to-all(bf16[16,4,16,512]{3,2,1,0:T(8,128)(2,1)} %convert_element_type.45), channel_id=1, replica_groups=mesh['ga'=2,'ta'=4,'gy'=4] {'ta'}, dimensions={0} | all-to-all | bytes 2097152 | tf_op jit(solution)/shard_map/all_to_all | solution.py:96
  111.0 0.1 copy.30
  111.1 0.0 copy-start.1
  111.1 0.0 copy-done.7
  111.1 1.7 %fusion.8 = bf16[4,4,64,512]{3,2,1,0:T(8,128)(2,1)} fusion(bf16[4,4,64,512]{3,2,1,0:T(8,128)(2,1)S(1)} %get-tuple-element.11, bf16[4,4,64,512]{3,2,1,0:T(8,128)(2,1)S(1)} %bitcast.118, bf16[512,512]{1,0:T(8,128)(2,1)S(1)} %copy-done.7), kind=kOutput, calls=%fused_computation.15 | convolution fusion | flops 538443776 | bytes 3670016 | tf_op jit(solution)/shard_map/dot_general | solution.py:110
  112.7 0.0 copy-done.1
  (2 shorter events, 0.0 us)
Async XLA Ops:
  0.0 54.4 %copy-start = (bf16[512,1536]{1,0:T(8,128)(2,1)S(1)}, bf16[512,1536]{1,0:T(8,128)(2,1)}, u32[]{:S(2)}) copy-start(bf16[512,1536]{1,0:T(8,128)(2,1)} %param.9) | copy-start | bytes 4718596
  1.2 10.5 %collective-permute-start = (bf16[4,1,64,512]{3,2,1,0:T(8,128)(2,1)S(1)}, bf16[4,1,64,512]{3,2,1,0:T(8,128)(2,1)S(1)}, u32[]{:S(2)}, u32[]{:S(2)}) collective-permute-start(bf16[4,1,64,512]{3,2,1,0:T(8,128)(2,1)S(1)} %get-tuple-element.8), channel_id=1, source_target_pairs={{0,1},{1,2},{2,3},{4,5},{5,6},{6,7},{8,9},{9,10},{10,11},{12,13},{... | collective-permute-start | bytes 786440 | tf_op jit(solution)/shard_map/ppermute | solution.py:14
  6.2 9.8 %copy-start.2 = (bf16[4,4,64,512]{3,2,1,0:T(8,128)(2,1)S(1)}, bf16[4,4,64,512]{3,2,1,0:T(8,128)(2,1)}, u32[]{:S(2)}) copy-start(bf16[4,4,64,512]{3,2,1,0:T(8,128)(2,1)} %param.6) | copy-start | bytes 3145732
  6.2 9.8 %collective-permute-start.1 = (bf16[4,1,64,512]{3,2,1,0:T(8,128)(2,1)S(1)}, bf16[4,1,64,512]{3,2,1,0:T(8,128)(2,1)S(1)}, u32[]{:S(2)}, u32[]{:S(2)}) collective-permute-start(bf16[4,1,64,512]{3,2,1,0:T(8,128)(2,1)S(1)} %get-tuple-element.9), channel_id=1, source_target_pairs={{1,0},{2,1},{3,2},{5,4},{6,5},{7,6},{9,8},{10,9},{11,10},{13,12},{... | collective-permute-start | bytes 786440 | tf_op jit(solution)/shard_map/ppermute | solution.py:17
  7.6 9.3 %copy-start.4 = (bf16[3,3,512,512]{3,2,1,0:T(8,128)(2,1)S(1)}, bf16[3,3,512,512]{3,2,1,0:T(8,128)(2,1)}, u32[]{:S(2)}) copy-start(bf16[3,3,512,512]{3,2,1,0:T(8,128)(2,1)} %param.7) | copy-start | bytes 14155780
  21.9 2.8 %copy-start.5 = (bf16[3,512,512]{2,1,0:T(8,128)(2,1)S(1)}, bf16[3,512,512]{2,1,0:T(8,128)(2,1)}, u32[]{:S(2)}) copy-start(bf16[3,512,512]{2,1,0:T(8,128)(2,1)} %param.8) | copy-start | bytes 4718596
  23.4 2.8 %collective-permute-start.2 = (bf16[2,4,64,512]{3,2,1,0:T(8,128)(2,1)S(1)}, bf16[2,4,64,512]{3,2,1,0:T(8,128)(2,1)S(1)}, u32[]{:S(2)}, u32[]{:S(2)}) collective-permute-start(bf16[2,4,64,512]{3,2,1,0:T(8,128)(2,1)S(1)} %slice.124), channel_id=1, source_target_pairs={{0,4},{4,8},{8,12},{1,5},{5,9},{9,13},{2,6},{6,10},{10,14},{3,7},{... | collective-permute-start | bytes 1572872 | tf_op jit(solution)/shard_map/ppermute | solution.py:25
  26.9 1.0 copy-start.6
  70.8 17.7 %copy-start.3 = (bf16[16,4,16,8,64]{4,3,2,1,0:T(8,128)(2,1)S(1)}, bf16[16,4,16,8,64]{4,3,2,1,0:T(8,128)(2,1)}, u32[]{:S(2)}) copy-start(bf16[16,4,16,8,64]{4,3,2,1,0:T(8,128)(2,1)} %reshape.84) | copy-start | bytes 3145732
  92.9 18.2 %copy-start.7 = (bf16[512,512]{1,0:T(8,128)(2,1)S(1)}, bf16[512,512]{1,0:T(8,128)(2,1)}, u32[]{:S(2)}) copy-start(bf16[512,512]{1,0:T(8,128)(2,1)} %param.10) | copy-start | bytes 1572868
  111.1 1.7 %copy-start.1 = (bf16[512,1536]{1,0:T(8,128)(2,1)S(1)}, bf16[512,1536]{1,0:T(8,128)(2,1)}, u32[]{:S(2)}) copy-start(bf16[512,1536]{1,0:T(8,128)(2,1)} %param.9) | copy-start | bytes 4718596
where the time goes:
time: 113 us
  blocking collectives  42.7 us (38%)
  matrix products  20.3 us (18%)
  other arithmetic  19 us (17%)
  local copies, waits for them, and re-layouts  15.9 us (14%)
  starting transfers between devices  7.72 us (7%)
  waiting for transfers between devices  6.9 us (6%)
    all_to_all x1, blocking collectives, per_device(): lax.all_to_all(normed, 'ta', split_axis=2, concat_axis=0, tiled=True)  24.7 us
    all_to_all x1, blocking collectives, attend_back(): return lax.all_to_all(output, 'ta', split_axis=0, concat_axis=2, tiled=True)  18 us
    sub x1, other arithmetic, attend(): expo = jnp.exp(scores - peak)  17.7 us
    dot_general x9, matrix products, conv_space(): jnp.dot(window.reshape(-1, channels), w_space[row_off, col_off], preferre...  8.59 us
    ppermute x1, starting transfers between devices, padded_2(): lax.ppermute(lax.slice_in_dim(block, block.shape[dim] - width, None, axis...  4.97 us
    ppermute x1, waiting for transfers between devices, padded_2(): lax.ppermute(lax.slice_in_dim(block, 0, width, axis=dim), axis, backward)  4.27 us
    dot_general x1, matrix products, attend(): jnp.einsum('frwhd,grwhd->rwhfg', queries.reshape(shape), keyset.reshape(s...  4.11 us
    reshape x1, local copies, waits for them, and re-layouts, attend(): queries.reshape(shape)  3.9 us
  transfers between devices with their start and end apart: 3, of which 3 were waited for; matrix products, arithmetic and copies ran while one was open for 3% of the time, Pallas kernels for 0%

commit v1 on v0

--- a/solution.py
+++ b/solution.py
@@ -4,6 +4,28 @@
 from jax.sharding import PartitionSpec as P
 
 HEADS = 8
+
+
+def cut_along(x, dim, count):
+    before, after = (x.shape[:dim], x.shape[dim + 1 :])
+    return jnp.moveaxis(x.reshape(*before, count, -1, *after), dim, 0)
+
+
+def joined_along(parts, dim):
+    parts = jnp.moveaxis(parts, 0, dim)
+    shape = parts.shape
+    return parts.reshape(*shape[:dim], shape[dim] * shape[dim + 1], *shape[dim + 2 :])
+
+
+def rotated_exchange(shard, axis, split_dim, concat_dim):
+    size, position = (lax.axis_size(axis), lax.axis_index(axis))
+    blocks = cut_along(shard, split_dim, size)
+    outs = [blocks[position]]
+    for hop in range(1, size):
+        sent = blocks[(position + hop) % size]
+        outs.append(lax.ppermute(sent, axis, [(i, (i + hop) % size) for i in range(size)]))
+    blocks = jnp.stack(outs)[(position - jnp.arange(size)) % size]
+    return joined_along(blocks, concat_dim)
 
 
 def padded_2(block, sides, width):
@@ -103,9 +125,7 @@
     hidden = jax.nn.silu(conv_space(padded, w_space, height, width)).astype(jnp.bfloat16)
     earlier = from_behind(hidden[-2:], "ta", 1)
     mixed, normed = temporal_mix(clip, hidden, earlier, w_time, norm_gain)
-    queries, keyset, valueset = project(
-        lax.all_to_all(normed, "ta", split_axis=2, concat_axis=0, tiled=True), w_qkv
-    )
+    queries, keyset, valueset = project(rotated_exchange(normed, "ta", 2, 0), w_qkv)
     attended = attend_back(queries, keyset, valueset)
     projected = jnp.dot(
         attended.reshape(-1, channels), w_out, preferred_element_type=jnp.float32

time: 113 us -> 102 us (0.903)
  blocking collectives: 42.7 us -> 18.2 us
  other arithmetic: 19 us -> 4.82 us
  starting transfers between devices: 7.72 us -> 17.8 us
  waiting for transfers between devices: 6.9 us -> 16.4 us
  matrix products: 20.3 us -> 25.8 us
  local copies, waits for them, and re-layouts: 15.9 us -> 18.5 us
    all_to_all x1 -> x0, blocking collectives: 24.7 us -> none  [per_device(): lax.all_to_all(normed, 'ta', split_axis=2, concat_axis=0, tiled=True)]
    sub x1, other arithmetic: 17.7 us -> 3.42 us  [attend(): expo = jnp.exp(scores - peak)]
    ppermute x0 -> x3, waiting for transfers between devices: none -> 10.2 us  [rotated_exchange(): lax.ppermute(sent, axis, [(i, (i + hop) % size) for i in range(size)])]
    ppermute x0 -> x3, starting transfers between devices: none -> 10.1 us  [rotated_exchange(): lax.ppermute(sent, axis, [(i, (i + hop) % size) for i in range(size)])]
    dot_general x1, matrix products: 1.72 us -> 4.44 us  [attend(): jnp.einsum('rwhfg,grwhd->frwhd', probs, valueset.reshape(shape), preferre...]
    gather x0 -> x1, local copies, waits for them, and re-layouts: none -> 1.6 us  [rotated_exchange(): blocks = jnp.stack(outs)[(position - jnp.arange(size)) % size]]
    dot_general x3, matrix products: 2.4 us -> 3.93 us  [temporal_mix(): jnp.dot(window.reshape(-1, channels), w_time[tap_index], preferred_elemen...]
    unnamed x16 -> x24, local copies, waits for them, and re-layouts: 0.04 us -> 1.55 us
  transfers between devices with their start and end apart: 3 -> 6, of which waited for: 3 -> 4; matrix products, arithmetic and copies ran while one was open for 3% -> 4% of each run, Pallas kernels for 0% -> 0%
where the time goes in v1:
time: 102 us
  matrix products  25.8 us (25%)
  local copies, waits for them, and re-layouts  18.5 us (18%)
  blocking collectives  18.2 us (18%)
  starting transfers between devices  17.8 us (17%)
  waiting for transfers between devices  16.4 us (16%)
  other arithmetic  4.82 us (5%)
    all_to_all x1, blocking collectives, attend_back(): return lax.all_to_all(output, 'ta', split_axis=0, concat_axis=2, tiled=True)  18.2 us
    ppermute x3, waiting for transfers between devices, rotated_exchange(): lax.ppermute(sent, axis, [(i, (i + hop) % size) for i in range(size)])  10.2 us
    ppermute x3, starting transfers between devices, rotated_exchange(): lax.ppermute(sent, axis, [(i, (i + hop) % size) for i in range(size)])  10.1 us
    dot_general x9, matrix products, conv_space(): jnp.dot(window.reshape(-1, channels), w_space[row_off, col_off], preferre...  8.59 us
    ppermute x1, starting transfers between devices, padded_2(): lax.ppermute(lax.slice_in_dim(block, block.shape[dim] - width, None, axis...  4.97 us
    dot_general x1, matrix products, attend(): jnp.einsum('rwhfg,grwhd->frwhd', probs, valueset.reshape(shape), preferre...  4.44 us
    ppermute x1, waiting for transfers between devices, padded_2(): lax.ppermute(lax.slice_in_dim(block, 0, width, axis=dim), axis, backward)  4.27 us
    dot_general x1, matrix products, attend(): jnp.einsum('frwhd,grwhd->rwhfg', queries.reshape(shape), keyset.reshape(s...  4.11 us
  transfers between devices with their start and end apart: 6, of which 4 were waited for; matrix products, arithmetic and copies ran while one was open for 4% of the time, Pallas kernels for 0%

profile of v1, /device:TPU:0, one launch (start us, length us, event | category | flops | bytes accessed | tf_op | source)
XLA Modules:
  0.0 101.8 jit_solution(7040172855501218752)
XLA Ops:
  0.0 0.0 copy-start
  0.0 1.2 %fusion.81 = (bf16[4,1,64,512]{3,2,1,0:T(8,128)(2,1)S(1)}, bf16[4,1,64,512]{3,2,1,0:T(8,128)(2,1)S(1)}) fusion(bf16[4,4,64,512]{3,2,1,0:T(8,128)(2,1)} %param.6), kind=kLoop, calls=%fused_computation.100 | loop fusion | bytes 1048576 | tf_op jit(solution)/shard_map/slice | solution.py:37
  1.2 5.0 %collective-permute-start = (bf16[4,1,64,512]{3,2,1,0:T(8,128)(2,1)S(1)}, bf16[4,1,64,512]{3,2,1,0:T(8,128)(2,1)S(1)}, u32[]{:S(2)}, u32[]{:S(2)}) collective-permute-start(bf16[4,1,64,512]{3,2,1,0:T(8,128)(2,1)S(1)} %get-tuple-element.12), channel_id=1, source_target_pairs={{0,1},{1,2},{2,3},{4,5},{5,6},{6,7},{8,9},{9,10},{10,11},{12,13},{... | collective-permute-start | bytes 786440 | tf_op jit(solution)/shard_map/ppermute | solution.py:36
  6.2 0.0 copy-start.2
  6.2 1.4 %collective-permute-start.1 = (bf16[4,1,64,512]{3,2,1,0:T(8,128)(2,1)S(1)}, bf16[4,1,64,512]{3,2,1,0:T(8,128)(2,1)S(1)}, u32[]{:S(2)}, u32[]{:S(2)}) collective-permute-start(bf16[4,1,64,512]{3,2,1,0:T(8,128)(2,1)S(1)} %get-tuple-element.13), channel_id=1, source_target_pairs={{1,0},{2,1},{3,2},{5,4},{6,5},{7,6},{9,8},{10,9},{11,10},{13,12},{... | collective-permute-start | bytes 786440 | tf_op jit(solution)/shard_map/ppermute | solution.py:39
  7.6 0.0 copy-start.8
  7.6 2.2 %fusion.55 = f32[4,4,64,512]{3,2,1,0:T(8,128)S(1)} fusion(bf16[4,4,64,512]{3,2,1,0:T(8,128)(2,1)} %param.6, bf16[3,3,512,512]{3,2,1,0:T(8,128)(2,1)} %param.7), kind=kOutput, calls=%fused_computation.64 | convolution fusion | flops 536870912 | bytes 3670016 | tf_op jit(solution)/shard_map/dot_general | solution.py:56
  9.8 1.9 %collective-permute-done = bf16[4,1,64,512]{3,2,1,0:T(8,128)(2,1)S(1)} collective-permute-done((bf16[4,1,64,512]{3,2,1,0:T(8,128)(2,1)S(1)}, bf16[4,1,64,512]{3,2,1,0:T(8,128)(2,1)S(1)}, u32[]{:S(2)}, u32[]{:S(2)}) %collective-permute-start) | collective-permute-done | bytes 262176 | tf_op jit(solution)/shard_map/ppermute | solution.py:36
  11.7 4.3 %collective-permute-done.1 = bf16[4,1,64,512]{3,2,1,0:T(8,128)(2,1)S(1)} collective-permute-done((bf16[4,1,64,512]{3,2,1,0:T(8,128)(2,1)S(1)}, bf16[4,1,64,512]{3,2,1,0:T(8,128)(2,1)S(1)}, u32[]{:S(2)}, u32[]{:S(2)}) %collective-permute-start.1) | collective-permute-done | bytes 262176 | tf_op jit(solution)/shard_map/ppermute | solution.py:39
  16.0 0.0 copy-done.2
  16.0 0.9 fusion.22
  16.9 0.0 copy-done.8
  16.9 0.7 fusion.35
  17.6 0.7 fusion.37
  18.3 0.7 fusion.39
  19.0 0.7 fusion.41
  19.8 0.7 fusion.43
  20.5 0.7 fusion.23
  21.2 0.7 fusion.27
  21.9 1.4 %multiply_convert_fusion = bf16[4,4,64,512]{3,2,1,0:T(8,128)(2,1)S(1)} fusion(f32[4,4,64,512]{3,2,1,0:T(8,128)S(1)} %fusion.27, f32[4,4,64,512]{3,2,1,0:T(8,128)S(1)} %fusion.35, f32[4,4,64,512]{3,2,1,0:T(8,128)S(1)} %fusion.37, f32[4,4,64,512]{3,2,1,0:T(8,128)S(1)} %fusion.55, f32[4,4,64,512]{3,2,1,0:T(8,128)S(1)} %fusion.39, ...), kind=kOutput, calls=%fused_computation.26 | convolution fusion | flops 543686656 | bytes 19398656 | tf_op jit(solution)/shard_map/dot_general | solution.py:56
  23.3 0.0 copy-start.3
  23.4 1.0 copy-done.3
  24.3 0.8 slice.126
  25.2 1.3 %collective-permute-start.2 = (bf16[2,4,64,512]{3,2,1,0:T(8,128)(2,1)}, bf16[2,4,64,512]{3,2,1,0:T(8,128)(2,1)S(1)}, u32[]{:S(2)}, u32[]{:S(2)}) collective-permute-start(bf16[2,4,64,512]{3,2,1,0:T(8,128)(2,1)} %slice.126), channel_id=1, source_target_pairs={{0,4},{4,8},{8,12},{1,5},{5,9},{9,13},{2,6},{6,10},{10,14},{3,7},{... | collective-permute-start | bytes 1572872 | tf_op jit(solution)/shard_map/ppermute | solution.py:47
  26.5 0.0 copy-start.4
  26.5 0.0 copy-start.9
  26.5 2.2 %fusion.49 = f32[4,4,64,512]{3,2,1,0:T(8,128)S(1)} fusion(bf16[4,4,64,512]{3,2,1,0:T(8,128)(2,1)} %copy-done.3, bf16[3,512,512]{2,1,0:T(8,128)(2,1)} %param.8), kind=kOutput, calls=%fused_computation.58 | convolution fusion | flops 536870912 | bytes 3670016 | tf_op jit(solution)/shard_map/dot_general | solution.py:72
  28.8 0.0 collective-permute-done.2
  28.8 0.0 copy-done.4
  28.8 0.0 copy-done.9
  28.8 0.7 fusion.45
  29.5 0.0 copy-start.10
  29.5 1.0 %fusion.5 = (f32[4,4,64]{2,1,0:T(4,128)S(1)}, bf16[4,4,64,512]{3,2,1,0:T(8,128)(2,1)S(1)}) fusion(bf16[3,512,512]{2,1,0:T(8,128)(2,1)S(1)} %copy-done.9, bf16[4,4,64,512]{3,2,1,0:T(8,128)(2,1)S(1)} %copy-done.4, bf16[2,4,64,512]{3,2,1,0:T(8,128)(2,1)S(1)} %collective-permute-done.2, f32[4,4,64,512]{3,2,1,0:T(8,128)S(1)} %fusion.49, ...), kind=kOutput, calls=%fused_computation.13 | convolution fusion | flops 544209920 | bytes 8392704 | tf_op jit(solution)/shard_map/dot_general | solution.py:72
  30.5 0.0 copy-start.5
  30.6 0.0 copy-done.10
  30.6 0.3 fusion.7
  30.9 0.1 dynamic-slice_bitcast_fusion.3
  31.0 0.5 copy-done.5
  31.5 6.3 %collective-permute-start.3 = (bf16[4,4,16,512]{3,2,1,0:T(8,128)(2,1)S(1)}, bf16[4,4,16,512]{3,2,1,0:T(8,128)(2,1)S(1)}, u32[]{:S(2)}, u32[]{:S(2)}) collective-permute-start(bf16[4,4,16,512]{3,2,1,0:T(8,128)(2,1)S(1)} %get-tuple-element.11), channel_id=1, source_target_pairs={{0,4},{4,8},{8,12},{12,0},{1,5},{5,9},{9,13},{13,1},{2,6},{6,10},{... | collective-permute-start | bytes 786440 | tf_op jit(solution)/shard_map/ppermute | solution.py:26
  37.8 2.3 %collective-permute-start.4 = (bf16[4,4,16,512]{3,2,1,0:T(8,128)(2,1)S(1)}, bf16[4,4,16,512]{3,2,1,0:T(8,128)(2,1)S(1)}, u32[]{:S(2)}, u32[]{:S(2)}) collective-permute-start(bf16[4,4,16,512]{3,2,1,0:T(8,128)(2,1)S(1)} %get-tuple-element.10), channel_id=1, source_target_pairs={{0,8},{4,12},{8,0},{12,4},{1,9},{5,13},{9,1},{13,5},{2,10},{6,14},... | collective-permute-start | bytes 786440 | tf_op jit(solution)/shard_map/ppermute | solution.py:26
  40.1 1.5 %collective-permute-start.5 = (bf16[4,4,16,512]{3,2,1,0:T(8,128)(2,1)S(1)}, bf16[4,4,16,512]{3,2,1,0:T(8,128)(2,1)S(1)}, u32[]{:S(2)}, u32[]{:S(2)}) collective-permute-start(bf16[4,4,16,512]{3,2,1,0:T(8,128)(2,1)S(1)} %get-tuple-element.9), channel_id=1, source_target_pairs={{0,12},{4,0},{8,4},{12,8},{1,13},{5,1},{9,5},{13,9},{2,14},{6,2},{... | collective-permute-start | bytes 786440 | tf_op jit(solution)/shard_map/ppermute | solution.py:26
  41.6 0.0 collective-permute-done.3
  41.6 5.2 %collective-permute-done.4 = bf16[4,4,16,512]{3,2,1,0:T(8,128)(2,1)S(1)} collective-permute-done((bf16[4,4,16,512]{3,2,1,0:T(8,128)(2,1)S(1)}, bf16[4,4,16,512]{3,2,1,0:T(8,128)(2,1)S(1)}, u32[]{:S(2)}, u32[]{:S(2)}) %collective-permute-start.4) | collective-permute-done | bytes 262176 | tf_op jit(solution)/shard_map/ppermute | solution.py:26
  46.8 5.0 %collective-permute-done.5 = bf16[4,4,16,512]{3,2,1,0:T(8,128)(2,1)S(1)} collective-permute-done((bf16[4,4,16,512]{3,2,1,0:T(8,128)(2,1)S(1)}, bf16[4,4,16,512]{3,2,1,0:T(8,128)(2,1)S(1)}, u32[]{:S(2)}, u32[]{:S(2)}) %collective-permute-start.5) | collective-permute-done | bytes 262176 | tf_op jit(solution)/shard_map/ppermute | solution.py:26
  51.8 0.1 pad_maximum_fusion.1
  52.0 1.6 %gather_fusion = bf16[4,4,4,16,512]{4,3,2,1,0:T(8,128)(2,1)} fusion(bf16[4,4,4,16,512]{4,3,2,1,0:T(8,128)(2,1)S(1)} %pad_maximum_fusion.1, s32[1024]{0:T(1024)S(1)} %pad_clamp_fusion), kind=kCustom, calls=%fused_computation | custom fusion | bytes 2097168 | tf_op jit(solution)/shard_map/gather | solution.py:27
  53.6 0.0 copy-done
  53.6 3.0 %convolution_convert_fusion = bf16[1024,1536]{1,0:T(8,128)(2,1)S(1)} fusion(bf16[1024,512]{1,0:T(8,128)(2,1)} %bitcast.129, bf16[512,1536]{1,0:T(8,128)(2,1)S(1)} %copy-done), kind=kOutput, calls=%fused_computation.6 | convolution fusion | flops 1612185600 | bytes 5767168 | tf_op jit(solution)/shard_map/dot_general | solution.py:85
  56.6 1.8 %fusion.80 = (bf16[16,4,16,512]{3,2,1,0:T(8,128)(2,1)}, bf16[16,4,16,512]{3,2,1,0:T(8,128)(2,1)}, bf16[16,4,16,512]{3,2,1,0:T(8,128)(2,1)}) fusion(bf16[16,4,16,1536]{3,2,1,0:T(8,128)(2,1)S(1)} %bitcast.128), kind=kLoop, calls=%fused_computation.99 | loop fusion | bytes 6291456 | tf_op jit(solution)/shard_map/slice | solution.py:92
  58.3 2.8 %reshape.140 = bf16[16,4,16,8,64]{4,3,2,1,0:T(8,128)(2,1)S(1)} reshape(bf16[16,4,16,512]{3,2,1,0:T(8,128)(2,1)} %get-tuple-element.7) | data formatting | bytes 2097152 | tf_op jit(solution)/shard_map/reshape | solution.py:102
  61.1 3.9 %reshape.141 = bf16[16,4,16,8,64]{4,3,2,1,0:T(8,128)(2,1)} reshape(bf16[16,4,16,512]{3,2,1,0:T(8,128)(2,1)} %get-tuple-element.6) | data formatting | bytes 2097152 | tf_op jit(solution)/shard_map/reshape | solution.py:103
  65.0 4.1 %fusion.11 = f32[4,16,8,16,16]{3,4,2,1,0:T(8,128)S(1)} fusion(bf16[16,4,16,8,64]{4,3,2,1,0:T(8,128)(2,1)} %reshape.141, bf16[16,4,16,8,64]{4,3,2,1,0:T(8,128)(2,1)S(1)} %reshape.140), kind=kOutput, calls=%fused_computation.19 | convolution fusion | flops 16777216 | bytes 2621440 | tf_op jit(solution)/shard_map/frwhd,grwhd->rwhfg/dot_general | solution.py:100
  69.1 3.4 %fusion.82 = (f32[4,16,8,16]{3,2,1,0:T(8,128)S(1)}, f32[4,16,8,16,16]{3,4,2,1,0:T(8,128)}) fusion(f32[4,16,8,16,16]{3,4,2,1,0:T(8,128)S(1)} %fusion.11), kind=kOutput, calls=%fused_computation.101 | output fusion | flops 524303 | bytes 1081344 | tf_op jit(solution)/shard_map/sub | solution.py:108
  72.6 0.0 copy-done.7
  72.6 2.1 %reshape.139 = bf16[16,4,16,8,64]{4,3,2,1,0:T(8,128)(2,1)} reshape(bf16[16,4,16,512]{3,2,1,0:T(8,128)(2,1)S(1)} %copy-done.7) | data formatting | bytes 2097152 | tf_op jit(solution)/shard_map/reshape | solution.py:111
  74.7 4.4 %convert_bitcast_fusion = bf16[16,4,16,8,64]{4,0,3,2,1:T(8,128)(2,1)S(1)} fusion(f32[4,16,8,16,16]{3,4,2,1,0:T(8,128)} %get-tuple-element.17, f32[4,16,8,16]{3,2,1,0:T(8,128)S(1)} %get-tuple-element.16, bf16[16,4,16,8,64]{4,3,2,1,0:T(8,128)(2,1)} %reshape.139), kind=kOutput, calls=%fused_computation.22 | convolution fusion | flops 17563648 | bytes 2654208 | tf_op jit(solution)/shard_map/rwhfg,grwhd->frwhd/dot_general | solution.py:110
  79.1 0.5 copy.12
  79.7 2.1 %convert_element_type.45 = bf16[16,4,16,512]{3,2,1,0:T(8,128)(2,1)} reshape(bf16[16,4,16,8,64]{4,3,2,1,0:T(8,128)(2,1)S(1)} %copy.12) | data formatting | bytes 2097152 | tf_op jit(solution)/shard_map/convert_element_type | solution.py:113
  81.7 18.2 %all_to_all.15 = bf16[16,4,16,512]{3,2,1,0:T(8,128)(2,1)S(1)} all-to-all(bf16[16,4,16,512]{3,2,1,0:T(8,128)(2,1)} %convert_element_type.45), channel_id=1, replica_groups=mesh['ga'=2,'ta'=4,'gy'=4] {'ta'}, dimensions={0} | all-to-all | bytes 2097152 | tf_op jit(solution)/shard_map/all_to_all | solution.py:118
  99.9 0.1 copy.13
  100.0 0.0 copy-start.1
  100.0 0.0 copy-done.6
  100.1 1.7 %fusion.8 = bf16[4,4,64,512]{3,2,1,0:T(8,128)(2,1)} fusion(bf16[4,4,64,512]{3,2,1,0:T(8,128)(2,1)S(1)} %copy-done.6, bf16[4,4,64,512]{3,2,1,0:T(8,128)(2,1)S(1)} %bitcast.130, bf16[512,512]{1,0:T(8,128)(2,1)S(1)} %copy-done.11), kind=kOutput, calls=%fused_computation.16 | convolution fusion | flops 538443776 | bytes 3670016 | tf_op jit(solution)/shard_map/dot_general | solution.py:130
  101.7 0.0 copy-done.1
  (7 shorter events, 0.0 us)
Async XLA Ops:
  0.0 53.6 %copy-start = (bf16[512,1536]{1,0:T(8,128)(2,1)S(1)}, bf16[512,1536]{1,0:T(8,128)(2,1)}, u32[]{:S(2)}) copy-start(bf16[512,1536]{1,0:T(8,128)(2,1)} %param.9) | copy-start | bytes 4718596
  1.2 10.5 %collective-permute-start = (bf16[4,1,64,512]{3,2,1,0:T(8,128)(2,1)S(1)}, bf16[4,1,64,512]{3,2,1,0:T(8,128)(2,1)S(1)}, u32[]{:S(2)}, u32[]{:S(2)}) collective-permute-start(bf16[4,1,64,512]{3,2,1,0:T(8,128)(2,1)S(1)} %get-tuple-element.12), channel_id=1, source_target_pairs={{0,1},{1,2},{2,3},{4,5},{5,6},{6,7},{8,9},{9,10},{10,11},{12,13},{... | collective-permute-start | bytes 786440 | tf_op jit(solution)/shard_map/ppermute | solution.py:36
  6.2 9.8 %copy-start.2 = (bf16[4,4,64,512]{3,2,1,0:T(8,128)(2,1)S(1)}, bf16[4,4,64,512]{3,2,1,0:T(8,128)(2,1)}, u32[]{:S(2)}) copy-start(bf16[4,4,64,512]{3,2,1,0:T(8,128)(2,1)} %param.6) | copy-start | bytes 3145732
  6.2 9.8 %collective-permute-start.1 = (bf16[4,1,64,512]{3,2,1,0:T(8,128)(2,1)S(1)}, bf16[4,1,64,512]{3,2,1,0:T(8,128)(2,1)S(1)}, u32[]{:S(2)}, u32[]{:S(2)}) collective-permute-start(bf16[4,1,64,512]{3,2,1,0:T(8,128)(2,1)S(1)} %get-tuple-element.13), channel_id=1, source_target_pairs={{1,0},{2,1},{3,2},{5,4},{6,5},{7,6},{9,8},{10,9},{11,10},{13,12},{... | collective-permute-start | bytes 786440 | tf_op jit(solution)/shard_map/ppermute | solution.py:39
  7.6 9.3 %copy-start.8 = (bf16[3,3,512,512]{3,2,1,0:T(8,128)(2,1)S(1)}, bf16[3,3,512,512]{3,2,1,0:T(8,128)(2,1)}, u32[]{:S(2)}) copy-start(bf16[3,3,512,512]{3,2,1,0:T(8,128)(2,1)} %param.7) | copy-start | bytes 14155780
  23.3 1.0 copy-start.3
  25.2 3.6 %collective-permute-start.2 = (bf16[2,4,64,512]{3,2,1,0:T(8,128)(2,1)}, bf16[2,4,64,512]{3,2,1,0:T(8,128)(2,1)S(1)}, u32[]{:S(2)}, u32[]{:S(2)}) collective-permute-start(bf16[2,4,64,512]{3,2,1,0:T(8,128)(2,1)} %slice.126), channel_id=1, source_target_pairs={{0,4},{4,8},{8,12},{1,5},{5,9},{9,13},{2,6},{6,10},{10,14},{3,7},{... | collective-permute-start | bytes 1572872 | tf_op jit(solution)/shard_map/ppermute | solution.py:47
  26.5 2.2 %copy-start.4 = (bf16[4,4,64,512]{3,2,1,0:T(8,128)(2,1)S(1)}, bf16[4,4,64,512]{3,2,1,0:T(8,128)(2,1)}, u32[]{:S(2)}) copy-start(bf16[4,4,64,512]{3,2,1,0:T(8,128)(2,1)} %copy-done.3) | copy-start | bytes 3145732
  26.5 2.2 %copy-start.9 = (bf16[3,512,512]{2,1,0:T(8,128)(2,1)S(1)}, bf16[3,512,512]{2,1,0:T(8,128)(2,1)}, u32[]{:S(2)}) copy-start(bf16[3,512,512]{2,1,0:T(8,128)(2,1)} %param.8) | copy-start | bytes 4718596
  29.5 1.1 %copy-start.10 = (f32[512]{0:T(512)S(1)}, f32[512]{0:T(512)}, u32[]{:S(2)}) copy-start(f32[512]{0:T(512)} %param.11) | copy-start | bytes 6148
  30.5 1.0 copy-start.5
  31.5 10.1 %collective-permute-start.3 = (bf16[4,4,16,512]{3,2,1,0:T(8,128)(2,1)S(1)}, bf16[4,4,16,512]{3,2,1,0:T(8,128)(2,1)S(1)}, u32[]{:S(2)}, u32[]{:S(2)}) collective-permute-start(bf16[4,4,16,512]{3,2,1,0:T(8,128)(2,1)S(1)} %get-tuple-element.11), channel_id=1, source_target_pairs={{0,4},{4,8},{8,12},{12,0},{1,5},{5,9},{9,13},{13,1},{2,6},{6,10},{... | collective-permute-start | bytes 786440 | tf_op jit(solution)/shard_map/ppermute | solution.py:26
  37.8 9.0 %collective-permute-start.4 = (bf16[4,4,16,512]{3,2,1,0:T(8,128)(2,1)S(1)}, bf16[4,4,16,512]{3,2,1,0:T(8,128)(2,1)S(1)}, u32[]{:S(2)}, u32[]{:S(2)}) collective-permute-start(bf16[4,4,16,512]{3,2,1,0:T(8,128)(2,1)S(1)} %get-tuple-element.10), channel_id=1, source_target_pairs={{0,8},{4,12},{8,0},{12,4},{1,9},{5,13},{9,1},{13,5},{2,10},{6,14},... | collective-permute-start | bytes 786440 | tf_op jit(solution)/shard_map/ppermute | solution.py:26
  40.1 11.7 %collective-permute-start.5 = (bf16[4,4,16,512]{3,2,1,0:T(8,128)(2,1)S(1)}, bf16[4,4,16,512]{3,2,1,0:T(8,128)(2,1)S(1)}, u32[]{:S(2)}, u32[]{:S(2)}) collective-permute-start(bf16[4,4,16,512]{3,2,1,0:T(8,128)(2,1)S(1)} %get-tuple-element.9), channel_id=1, source_target_pairs={{0,12},{4,0},{8,4},{12,8},{1,13},{5,1},{9,5},{13,9},{2,14},{6,2},{... | collective-permute-start | bytes 786440 | tf_op jit(solution)/shard_map/ppermute | solution.py:26
  69.1 3.4 %copy-start.7 = (bf16[16,4,16,512]{3,2,1,0:T(8,128)(2,1)S(1)}, bf16[16,4,16,512]{3,2,1,0:T(8,128)(2,1)}, u32[]{:S(2)}) copy-start(bf16[16,4,16,512]{3,2,1,0:T(8,128)(2,1)} %get-tuple-element.5) | copy-start | bytes 3145732
  81.7 18.3 %copy-start.6 = (bf16[4,4,64,512]{3,2,1,0:T(8,128)(2,1)S(1)}, bf16[4,4,64,512]{3,2,1,0:T(8,128)(2,1)}, u32[]{:S(2)}) copy-start(bf16[4,4,64,512]{3,2,1,0:T(8,128)(2,1)} %copy-done.5) | copy-start | bytes 3145732
  81.7 18.3 %copy-start.11 = (bf16[512,512]{1,0:T(8,128)(2,1)S(1)}, bf16[512,512]{1,0:T(8,128)(2,1)}, u32[]{:S(2)}) copy-start(bf16[512,512]{1,0:T(8,128)(2,1)} %param.10) | copy-start | bytes 1572868
  100.0 1.7 %copy-start.1 = (bf16[512,1536]{1,0:T(8,128)(2,1)S(1)}, bf16[512,1536]{1,0:T(8,128)(2,1)}, u32[]{:S(2)}) copy-start(bf16[512,1536]{1,0:T(8,128)(2,1)} %param.9) | copy-start | bytes 4718596
